TPU v7x, 32 devices: a whole 2x2x4 slice. The times are simulated.
32 devices in a mesh: groups: 2 (over y), seq: 4 (over z), exp: 2 (over x), tp: 2 (over core).
Axes of the slice: x: 2, y: 2, z: 4, core: 2. Of those that a mesh axis runs over, the one named last changes fastest.
Arguments:
- attn_query: bfloat16 [2048, 1152], P(('groups', 'seq'), ('exp', 'tp')), parts along dimension 0, may hold values from -6 to 6
- fresh_keys: bfloat16 [2048, 1152], P(('groups', 'seq'), ('exp', 'tp')), parts along dimension 0, may hold values from -6 to 6
- fresh_values: bfloat16 [2048, 1152], P(('groups', 'seq'), ('exp', 'tp')), parts along dimension 0, may hold values from -6 to 6
- stale_keys: bfloat16 [2048, 1152], P(('groups', 'seq'), ('exp', 'tp')), parts along dimension 0, may hold values from -6 to 6
- stale_values: bfloat16 [2048, 1152], P(('groups', 'seq'), ('exp', 'tp')), parts along dimension 0, may hold values from -6 to 6
- block_flags: int32 [16], P(('groups', 'seq')), parts along dimension 0, may hold values 0 or 1
- moe_tokens: bfloat16 [4096, 1152], P(('groups', 'seq', 'exp', 'tp')), parts along dimension 0, may hold values from -6 to 6
- expert_ids: int32 [4096, 2], P(('groups', 'seq', 'exp', 'tp')), parts along dimension 0, may hold values from 0 to 3, all different within a row; in each aligned block of 128 rows (0 to 127, 128 to 255, ...) at most 80 rows name the same one
- gate_weights: float32 [4096, 2], P(('groups', 'seq', 'exp', 'tp')), parts along dimension 0, may hold values from 0.25 to 1
- up_weight: bfloat16 [4, 1152, 4608], P('seq', None, ('exp', 'tp')), may hold values from -0.1875 to 0.1875
- up_bias: float32 [4, 4608], P('seq', ('exp', 'tp')), may hold values from -3 to 3
- down_weight: bfloat16 [4, 4608, 1152], P('seq', ('exp', 'tp')), may hold values from -0.09375 to 0.09375
- down_bias: float32 [4, 1152], P('seq'), may hold values from -2 to 2
Outputs:
- attn_out: bfloat16 [2048, 1152], P(('groups', 'seq'), ('exp', 'tp')), parts along dimension 0
- moe_out: bfloat16 [4096, 1152], P(('groups', 'seq', 'exp', 'tp')), parts along dimension 0
There are 2 independent parts, one for each index of `groups`. A program takes and returns all parts, laid end to end along the dimension named above; an argument that names none is the same for every part. Nothing has to cross between parts.
Inputs may be any that keep to these rules, and one draw needn't show every extreme that they name: `expert_ids`: the 2 ids of a token differ. In the rows of one device no expert is named more than 80 times, and in every draw some expert is named exactly 80 times in some device's rows.
All inputs are finite; a program needn't handle non-finite values. No bound on the sum of `block_flags` on one device may be relied on, other than what follows from the above.
Results may differ from a plain program's by a relative error of at most 0.014.
Values may be sent and summed in bfloat16 or wider, within the bound.
A program may use at most 64 MiB of HBM per device.

v0:
```python
import math
import jax
import jax.numpy as jnp
from jax import lax
from jax.sharding import PartitionSpec as P

HD = 72


def over_all_2(share, axis, dim, apply):
    everything = lax.all_gather(share, axis, axis=dim, tiled=True)
    return apply(everything, jnp.int32(0))


def attention_part(attn_query, fresh_keys, fresh_values, stale_keys, stale_values, block_flags):
    length = attn_query.shape[0]
    heads_here = attn_query.shape[1] // HD
    row_flags = (jnp.repeat(block_flags, length // block_flags.shape[0]) == 1)[:, None]
    keys = jnp.where(row_flags, fresh_keys, stale_keys)
    values = jnp.where(row_flags, fresh_values, stale_values)
    queries = attn_query.reshape(length, heads_here, HD)
    scale = 1.0 / math.sqrt(HD)
    initial = (
        jnp.full((heads_here, length), -1e30, jnp.float32),
        jnp.zeros((heads_here, length), jnp.float32),
        jnp.zeros((heads_here, length, HD), jnp.float32),
    )
    carry = initial
    piece = (
        lax.all_gather(keys, "seq", axis=0, tiled=True),
        lax.all_gather(values, "seq", axis=0, tiled=True),
    )
    count = piece[0].shape[0]
    width = math.gcd(count, 512)
    key_blocks = piece[0].reshape(count // width, width, heads_here, HD)
    value_blocks = piece[1].reshape(count // width, width, heads_here, HD)

    def advance(state, blocks):
        highest, totals, weighted = state
        key_block, value_block = blocks
        scores = (
            jnp.einsum("qhd,khd->hqk", queries, key_block, preferred_element_type=jnp.float32)
            * scale
        )
        new_high = jnp.maximum(highest, jnp.max(scores, axis=-1))
        rescale = jnp.exp(highest - new_high)
        probs = jnp.exp(scores - new_high[:, :, None])
        totals = totals * rescale + jnp.sum(probs, axis=-1)
        weighted = weighted * rescale[:, :, None] + jnp.einsum(
            "hqk,khd->hqd",
            probs.astype(jnp.bfloat16),
            value_block,
            preferred_element_type=jnp.float32,
        )
        return ((new_high, totals, weighted), None)

    carry, unused = lax.scan(advance, carry, (key_blocks, value_blocks))
    highest, totals, weighted = carry
    mixed = weighted / totals[:, :, None]
    return jnp.transpose(mixed, (1, 0, 2)).reshape(length, heads_here * HD).astype(jnp.bfloat16)


def expert_part(moe_tokens, expert_ids, gate_weights, up_weight, up_bias, down_weight, down_bias):
    tokens_here, width = moe_tokens.shape
    choose = expert_ids.shape[1]
    number = lax.axis_size("seq") * up_weight.shape[0]
    capacity = 5 * tokens_here // (2 * number)
    flat_ids = expert_ids.reshape(-1)
    hits = (flat_ids[:, None] == jnp.arange(number, dtype=jnp.int32)[None, :]).astype(jnp.int32)
    before = jnp.cumsum(hits, axis=0) - hits
    place = jnp.sum(before * hits, axis=1)
    slot = flat_ids * capacity + place
    slot_pairs = slot.reshape(tokens_here, choose)
    table = jnp.sum(
        (
            slot_pairs[None, :, :] == jnp.arange(number * capacity, dtype=jnp.int32)[:, None, None]
        ).astype(jnp.int32),
        axis=-1,
    )
    buffer = jnp.dot(
        table.astype(jnp.bfloat16), moe_tokens, preferred_element_type=jnp.float32
    ).astype(jnp.bfloat16)
    buffer = buffer.reshape(number, capacity, width)
    received = lax.all_to_all(buffer, "seq", split_axis=0, concat_axis=0, tiled=True)
    sources = received.shape[0]
    count = received.shape[1]
    flat_rows = received.reshape(sources * count, width)
    chip_rows = lax.all_gather(flat_rows, "tp", axis=0, tiled=True)

    def project(piece):
        return jax.nn.gelu(
            jnp.dot(chip_rows, piece[0], preferred_element_type=jnp.float32) + piece[1]
        ).astype(jnp.bfloat16)

    hidden = over_all_2(
        (up_weight[0], up_bias[0][None, :].astype(jnp.bfloat16)),
        "exp",
        1,
        lambda piece, start: project((piece[0], piece[1].astype(jnp.float32))),
    )
    down_whole = lax.all_gather(down_weight[0], "exp", axis=0, tiled=True)
    summed = lax.psum_scatter(
        jnp.dot(hidden, down_whole, preferred_element_type=jnp.float32).astype(jnp.bfloat16),
        "tp",
        scatter_dimension=0,
        tiled=True,
    ).astype(jnp.float32)
    result = (summed + down_bias[0][None, :]).astype(jnp.bfloat16).reshape(sources, count, width)
    returned = lax.all_to_all(result, "seq", split_axis=0, concat_axis=0, tiled=True)
    flat_out = returned.reshape(number * capacity, width)
    picked = flat_out[slot].reshape(tokens_here, choose, width).astype(jnp.float32)
    combined = jnp.sum(picked * gate_weights[:, :, None], axis=1)
    return combined.astype(jnp.bfloat16)


def local(
    attn_query,
    fresh_keys,
    fresh_values,
    stale_keys,
    stale_values,
    block_flags,
    moe_tokens,
    expert_ids,
    gate_weights,
    up_weight,
    up_bias,
    down_weight,
    down_bias,
):
    attn_out = attention_part(
        attn_query, fresh_keys, fresh_values, stale_keys, stale_values, block_flags
    )
    moe_out = expert_part(
        moe_tokens, expert_ids, gate_weights, up_weight, up_bias, down_weight, down_bias
    )
    return (attn_out, moe_out)


def solution(mesh):
    in_specs = (
        P(("groups", "seq"), ("exp", "tp")),
        P(("groups", "seq"), ("exp", "tp")),
        P(("groups", "seq"), ("exp", "tp")),
        P(("groups", "seq"), ("exp", "tp")),
        P(("groups", "seq"), ("exp", "tp")),
        P(("groups", "seq")),
        P(("groups", "seq", "exp", "tp"), None),
        P(("groups", "seq", "exp", "tp"), None),
        P(("groups", "seq", "exp", "tp"), None),
        P("seq", None, ("exp", "tp")),
        P("seq", ("exp", "tp")),
        P("seq", ("exp", "tp"), None),
        P("seq", None),
    )
    out_specs = (P(("groups", "seq"), ("exp", "tp")), P(("groups", "seq", "exp", "tp"), None))
    return jax.shard_map(local, mesh=mesh, in_specs=in_specs, out_specs=out_specs, check_vma=False)
```

profile of v0, /device:TPU:0, one launch (start us, length us, event | category | flops | bytes accessed | tf_op | source)
XLA Modules:
  0.0 262.1 jit_solution(10440550585438227936)
XLA Ops:
  7.2 0.8 copy.32
  8.3 1.2 reduce-window.6
  10.6 25.3 %all_to_all.10 = bf16[4,80,1152]{2,1,0:T(8,128)(2,1)} all-to-all(bf16[4,80,1152]{2,1,0:T(8,128)(2,1)S(1)} %bitcast.82), channel_id=1, replica_groups=mesh['groups'=2,'seq'=4,'exp'=2,'tp'=2] {'seq'}, dimensions={0} | all-to-all | bytes 1474560 | tf_op jit(solution)/shard_map/all_to_all | solution.py:84
  36.0 0.7 all-gather.8.cloned.1.call-update
  37.5 4.4 %all_gather.22 = bf16[1,2304]{1,0:T(2,128)(2,1)S(1)} all-gather(bf16[1,1152]{1,0:T(2,128)(2,1)S(1)} %convert_element_type.61), channel_id=1, replica_groups=mesh['groups'=2,'seq'=4,'exp'=2,'tp'=2] {'exp'}, dimensions={1}, use_global_device_ids=true | all-gather | bytes 6912 | tf_op jit(solution)/shard_map/all_gather | solution.py:11
  41.9 3.0 %all-gather.6.cloned.1.call-done = bf16[640,1152]{1,0:T(8,128)(2,1)} async-done(((bf16[320,1152]{1,0:T(8,128)(2,1)}), bf16[640,1152]{1,0:T(8,128)(2,1)}) %all-gather.6.cloned.1.call-update) | async-done | bytes 1474576 | tf_op jit(solution)/shard_map/all_gather | solution.py:88
  44.9 72.0 %all-gather.8.cloned.1.call-done = bf16[1,1152,2304]{2,1,0:T(8,128)(2,1)} async-done(((bf16[1,1152,1152]{2,1,0:T(8,128)(2,1)}), bf16[1,1152,2304]{2,1,0:T(8,128)(2,1)}) %all-gather.8.cloned.1.call-update) | async-done | bytes 5308432 | tf_op jit(solution)/shard_map/all_gather | solution.py:11
  116.9 9.6 %fusion.22 = bf16[640,2304]{1,0:T(8,128)(2,1)} fusion(bf16[640,1152]{1,0:T(8,128)(2,1)} %all-gather.6.cloned.1.call-done, bf16[1,1152,2304]{2,1,0:T(8,128)(2,1)} %all-gather.8.cloned.1.call-done, f32[2304]{0:T(1024)S(1)} %convert_reduce_fusion.1), kind=kOutput, calls=%fused_computation.30 | convolution fusion | flops 3412131840 | bytes 9741312 | tf_op jit(solution)/shard_map/dot_general | solution.py:92
  126.5 61.3 %all-gather.10.cloned.1.call-done = bf16[1,2304,1152]{2,1,0:T(8,128)(2,1)} async-done(((bf16[1,1152,1152]{2,1,0:T(8,128)(2,1)}), bf16[1,2304,1152]{2,1,0:T(8,128)(2,1)}) %all-gather.10.cloned.1.call-update) | async-done | bytes 5308432 | tf_op jit(solution)/shard_map/all_gather | solution.py:101
  187.8 8.5 %fusion.29 = bf16[640,1152]{1,0:T(8,128)(2,1)} fusion(bf16[640,2304]{1,0:T(8,128)(2,1)} %fusion.22, bf16[1,2304,1152]{2,1,0:T(8,128)(2,1)} %all-gather.10.cloned.1.call-done), kind=kOutput, calls=%fused_computation.35 | convolution fusion | flops 3398123520 | bytes 9732096 | tf_op jit(solution)/shard_map/dot_general | solution.py:103
  196.5 16.5 %all_gather.18 = bf16[1024,288]{0,1:T(8,128)(2,1)S(1)} all-gather(bf16[256,288]{0,1:T(8,128)(2,1)S(1)} %get-tuple-element.101), channel_id=1, replica_groups=mesh['groups'=2,'seq'=4,'exp'=2,'tp'=2] {'seq'}, dimensions={0}, use_global_device_ids=true | all-gather | bytes 737280 | tf_op jit(solution)/shard_map/all_gather | solution.py:30
  213.5 0.9 copy.30
  214.4 16.1 %all_gather.19 = bf16[1024,288]{0,1:T(8,128)(2,1)S(1)} all-gather(bf16[256,288]{0,1:T(8,128)(2,1)S(1)} %get-tuple-element.100), channel_id=1, replica_groups=mesh['groups'=2,'seq'=4,'exp'=2,'tp'=2] {'seq'}, dimensions={0}, use_global_device_ids=true | all-gather | bytes 737280 | tf_op jit(solution)/shard_map/all_gather | solution.py:31
  230.9 0.9 copy.31
  231.9 2.1 add_convert_fusion
  234.0 4.9 %all-to-all-start.1 = ((bf16[4,80,1152]{2,1,0:T(8,128)(2,1)}), bf16[4,80,1152]{2,1,0:T(8,128)(2,1)S(1)}, u32[]{:S(2)}, u32[]{:S(2)}) async-start(bf16[4,80,1152]{2,1,0:T(8,128)(2,1)} %bitcast.10), calls=%async_computation.2 | async-start | bytes 1474560 | tf_op jit(solution)/shard_map/all_to_all | solution.py:109
  238.8 6.9 %while.15 = (s32[]{:T(128)}, f32[4,256]{1,0:T(4,128)S(1)}, f32[4,256]{1,0:T(4,128)S(1)}, f32[4,256,72]{1,2,0:T(8,128)S(1)}, bf16[2,512,4,72]{1,3,2,0:T(8,128)(2,...) while((s32[]{:T(128)}, f32[4,256]{1,0:T(4,128)S(1)}, ...), condition=%wide.region_3.4_spmd.clone, body=%wide.region_0.3_spmd.clone.sunk | while | flops 155415552 | bytes 7685225 | solution.py:57
  238.8 1.5 bitcast_reduce_fusion.2
  240.8 1.5 convolution_add_fusion.2
  242.3 1.5 bitcast_reduce_fusion.2
  244.2 1.5 convolution_add_fusion.2
  246.7 4.9 %all-to-all-done.1 = bf16[4,80,1152]{2,1,0:T(8,128)(2,1)S(1)} async-done(((bf16[4,80,1152]{2,1,0:T(8,128)(2,1)}), bf16[4,80,1152]{2,1,0:T(8,128)(2,1)S(1)}, u32[]{:S(2)}, u32[]{:S(2)}) %all-to-all-start.1) | async-done | bytes 737312 | tf_op jit(solution)/shard_map/all_to_all | solution.py:109
  251.6 1.3 gather_fusion
  253.4 2.2 multiply_reduce_fusion
  (66 shorter events, 5.6 us)
Async XLA Ops:
  7.2 3.1 %copy-start = (bf16[128,1152]{1,0:T(8,128)(2,1)S(1)}, bf16[128,1152]{1,0:T(8,128)(2,1)}, u32[]{:S(2)}) copy-start(bf16[128,1152]{1,0:T(8,128)(2,1)} %param.21) | copy-start | bytes 884740
  7.2 37.7 %all-gather.6.cloned.1.call-start = ((), (), s32[]{:S(2)}) async-start(), calls=%async_computation.3 | async-start | bytes 2211840 | tf_op jit(solution)/shard_map/all_gather | solution.py:88
  36.0 1.5 copy-start.5
  36.0 80.9 %all-gather.8.cloned.1.call-start = ((), (), s32[]{:S(2)}) async-start(), calls=%async_computation.5 | async-start | bytes 7962624 | tf_op jit(solution)/shard_map/all_gather | solution.py:11
  36.7 151.0 %all-gather.10.cloned.1.call-start = ((), (), s32[]{:S(2)}) async-start(), calls=%async_computation.6 | async-start | bytes 7962624 | tf_op jit(solution)/shard_map/all_gather | solution.py:101
  37.5 194.4 %reduce-scatter.2.cloned.1.call-start = ((), (), s32[]{:S(2)}) async-start(), calls=%async_computation.4 | async-start | bytes 2211840 | tf_op jit(solution)/shard_map/reduce_scatter | solution.py:102
  126.5 69.9 %copy-start.8 = (s32[2]{0:T(128)S(1)}, s32[2]{0:T(128)}, u32[]{:S(2)}) copy-start(s32[2]{0:T(128)} %param.20) | copy-start | bytes 28
  126.5 70.0 %copy-start.1 = (bf16[256,288]{0,1:T(8,128)(2,1)S(1)}, bf16[256,288]{0,1:T(8,128)(2,1)}, u32[]{:S(2)}) copy-start(bf16[256,288]{0,1:T(8,128)(2,1)} %param.17) | copy-start | bytes 442372
  126.5 70.0 %copy-start.2 = (bf16[256,288]{0,1:T(8,128)(2,1)S(1)}, bf16[256,288]{0,1:T(8,128)(2,1)}, u32[]{:S(2)}) copy-start(bf16[256,288]{0,1:T(8,128)(2,1)} %param.19) | copy-start | bytes 442372
  126.5 70.0 %copy-start.3 = (bf16[256,288]{0,1:T(8,128)(2,1)S(1)}, bf16[256,288]{0,1:T(8,128)(2,1)}, u32[]{:S(2)}) copy-start(bf16[256,288]{0,1:T(8,128)(2,1)} %param.16) | copy-start | bytes 442372
  126.5 70.0 %copy-start.4 = (bf16[256,288]{0,1:T(8,128)(2,1)S(1)}, bf16[256,288]{0,1:T(8,128)(2,1)}, u32[]{:S(2)}) copy-start(bf16[256,288]{0,1:T(8,128)(2,1)} %param.18) | copy-start | bytes 442372
  213.1 18.7 %copy-start.6 = (f32[1,1152]{1,0:T(1,128)S(1)}, f32[1,1152]{1,0:T(1,128)}, u32[]{:S(2)}) copy-start(f32[1,1152]{1,0:T(1,128)} %param.27) | copy-start | bytes 13828
  234.0 17.6 %all-to-all-start.1 = ((bf16[4,80,1152]{2,1,0:T(8,128)(2,1)}), bf16[4,80,1152]{2,1,0:T(8,128)(2,1)S(1)}, u32[]{:S(2)}, u32[]{:S(2)}) async-start(bf16[4,80,1152]{2,1,0:T(8,128)(2,1)} %bitcast.10), calls=%async_computation.2 | async-start | bytes 1474560 | tf_op jit(solution)/shard_map/all_to_all | solution.py:109
  238.8 7.0 %copy-start.7 = (f32[128,2]{0,1:T(2,128)S(1)}, f32[128,2]{0,1:T(2,128)}, u32[]{:S(2)}) copy-start(f32[128,2]{0,1:T(2,128)} %param.23) | copy-start | bytes 3076
Sparse Core Ops, SparseCore 0:
  36.1 8.7 all-gather.5
  46.4 70.4 all-gather.7
  118.5 69.2 all-gather.9
  196.5 8.9 reduce-scatter.1
where the time goes:
time: 263 us; the launch traced here: 262 us
  waiting for transfers between devices  143 us (54%)
  blocking collectives  62.3 us (24%)
  matrix products  24.4 us (9%)
  between operations  14 us (5%)
  other arithmetic  7.3 us (3%)
  local copies, waits for them, and re-layouts  6.41 us (2%)
  starting transfers between devices  5.02 us (2%)
    all_gather x1, waiting for transfers between devices, over_all_2(): everything = lax.all_gather(share, axis, axis=dim, tiled=True)  72 us
    all_gather x1, waiting for transfers between devices, expert_part(): down_whole = lax.all_gather(down_weight[0], 'exp', axis=0, tiled=True)  61.3 us
    all_to_all x1, blocking collectives, expert_part(): lax.all_to_all(buffer, 'seq', split_axis=0, concat_axis=0, tiled=True)  25.3 us
    all_gather x1, blocking collectives, attention_part(): lax.all_gather(keys, 'seq', axis=0, tiled=True)  16.5 us
    all_gather x1, blocking collectives, attention_part(): lax.all_gather(values, 'seq', axis=0, tiled=True)  16.1 us
    dot_general x1, matrix products, project(): jnp.dot(chip_rows, piece[0], preferred_element_type=jnp.float32) + piece[1]  9.57 us
    dot_general x1, matrix products, expert_part(): jnp.dot(hidden, down_whole, preferred_element_type=jnp.float32)  8.54 us
  transfers between devices with their start and end apart: 5, of which 4 were waited for; matrix products, arithmetic and copies ran while one was open for 8% of the time, Pallas kernels for 0%

commit v1 on v0

--- a/solution.py
+++ b/solution.py
@@ -5,6 +5,24 @@
 from jax.sharding import PartitionSpec as P
 
 HD = 72
+
+
+def collect(value, axis, dim):
+    ways, here, step = (lax.axis_size(axis), lax.axis_index(axis), value.shape[dim])
+    dims = [n * ways if d == dim else n for d, n in enumerate(value.shape)]
+    full = lax.dynamic_update_slice_in_dim(
+        jnp.zeros(dims, value.dtype), value, here * step, axis=dim
+    )
+    going_up = going_down = value
+    for far in range(1, ways // 2 + 1):
+        going_up = lax.ppermute(going_up, axis, [(d, (d + 1) % ways) for d in range(ways)])
+        full = lax.dynamic_update_slice_in_dim(full, going_up, (here - far) % ways * step, axis=dim)
+        if 2 * far < ways:
+            going_down = lax.ppermute(going_down, axis, [(d, (d - 1) % ways) for d in range(ways)])
+            full = lax.dynamic_update_slice_in_dim(
+                full, going_down, (here + far) % ways * step, axis=dim
+            )
+    return full
 
 
 def over_all_2(share, axis, dim, apply):
@@ -26,10 +44,7 @@
         jnp.zeros((heads_here, length, HD), jnp.float32),
     )
     carry = initial
-    piece = (
-        lax.all_gather(keys, "seq", axis=0, tiled=True),
-        lax.all_gather(values, "seq", axis=0, tiled=True),
-    )
+    piece = (collect(keys, "seq", 0), lax.all_gather(values, "seq", axis=0, tiled=True))
     count = piece[0].shape[0]
     width = math.gcd(count, 512)
     key_blocks = piece[0].reshape(count // width, width, heads_here, HD)

time: 263 us -> 260 us (0.989)
  blocking collectives: 62.3 us -> 47.7 us
  waiting for transfers between devices: 143 us -> 151 us
  starting transfers between devices: 5.02 us -> 8.43 us
    all_gather x1 -> x0, blocking collectives: 16.5 us -> none  [attention_part(): lax.all_gather(keys, 'seq', axis=0, tiled=True)]
    ppermute x0 -> x3, waiting for transfers between devices: none -> 6.22 us  [the longest x2 6.22 us: collect(): lax.ppermute(going_up, axis, [(d, (d + 1) % ways) for d in range(ways)])]
    ppermute x0 -> x3, starting transfers between devices: none -> 4.6 us  [the longest x1 2.34 us: collect(): lax.ppermute(going_down, axis, [(d, (d - 1) % ways) for d in range(ways)])]
  transfers between devices with their start and end apart: 5 -> 8, of which waited for: 4 -> 5; matrix products, arithmetic and copies ran while one was open for 8% -> 8% of each run, Pallas kernels for 0% -> 0%
where the time goes in v1:
time: 260 us
  waiting for transfers between devices  151 us (58%)
  blocking collectives  47.7 us (18%)
  matrix products  24.4 us (9%)
  between operations  14.1 us (5%)
  starting transfers between devices  8.43 us (3%)
  other arithmetic  7.36 us (3%)
  local copies, waits for them, and re-layouts  6.53 us (3%)
    all_gather x1, waiting for transfers between devices, over_all_2(): everything = lax.all_gather(share, axis, axis=dim, tiled=True)  72 us
    all_gather x1, waiting for transfers between devices, expert_part(): down_whole = lax.all_gather(down_weight[0], 'exp', axis=0, tiled=True)  61.2 us
    all_to_all x1, blocking collectives, expert_part(): lax.all_to_all(buffer, 'seq', split_axis=0, concat_axis=0, tiled=True)  25.3 us
    all_gather x1, blocking collectives, attention_part(): lax.all_gather(values, 'seq', axis=0, tiled=True)  18 us
    dot_general x1, matrix products, project(): jnp.dot(chip_rows, piece[0], preferred_element_type=jnp.float32) + piece[1]  9.58 us
    dot_general x1, matrix products, expert_part(): jnp.dot(hidden, down_whole, preferred_element_type=jnp.float32)  8.54 us
    all_to_all x1, waiting for transfers between devices, expert_part(): lax.all_to_all(result, 'seq', split_axis=0, concat_axis=0, tiled=True)  7.02 us
    ppermute x2, waiting for transfers between devices, collect(): lax.ppermute(going_up, axis, [(d, (d + 1) % ways) for d in range(ways)])  6.22 us
  transfers between devices with their start and end apart: 8, of which 5 were waited for; matrix products, arithmetic and copies ran while one was open for 8% of the time, Pallas kernels for 0%

profile of v1, /device:TPU:0, one launch (start us, length us, event | category | flops | bytes accessed | tf_op | source)
XLA Modules:
  0.0 259.5 jit_solution(17759264908889127979)
XLA Ops:
  8.3 1.2 reduce-window.6
  10.6 25.3 %all_to_all.10 = bf16[4,80,1152]{2,1,0:T(8,128)(2,1)} all-to-all(bf16[4,80,1152]{2,1,0:T(8,128)(2,1)S(1)} %bitcast.82), channel_id=1, replica_groups=mesh['groups'=2,'seq'=4,'exp'=2,'tp'=2] {'seq'}, dimensions={0} | all-to-all | bytes 1474560 | tf_op jit(solution)/shard_map/all_to_all | solution.py:99
  37.5 4.4 %all_gather.18 = bf16[1,2304]{1,0:T(2,128)(2,1)S(1)} all-gather(bf16[1,1152]{1,0:T(2,128)(2,1)S(1)} %convert_element_type.61), channel_id=1, replica_groups=mesh['groups'=2,'seq'=4,'exp'=2,'tp'=2] {'exp'}, dimensions={1}, use_global_device_ids=true | all-gather | bytes 6912 | tf_op jit(solution)/shard_map/all_gather | solution.py:29
  41.9 3.0 %all-gather.6.cloned.1.call-done = bf16[640,1152]{1,0:T(8,128)(2,1)} async-done(((bf16[320,1152]{1,0:T(8,128)(2,1)}), bf16[640,1152]{1,0:T(8,128)(2,1)}) %all-gather.6.cloned.1.call-update) | async-done | bytes 1474576 | tf_op jit(solution)/shard_map/all_gather | solution.py:103
  44.9 72.0 %all-gather.8.cloned.1.call-done = bf16[1,1152,2304]{2,1,0:T(8,128)(2,1)} async-done(((bf16[1,1152,1152]{2,1,0:T(8,128)(2,1)}), bf16[1,1152,2304]{2,1,0:T(8,128)(2,1)}) %all-gather.8.cloned.1.call-update) | async-done | bytes 5308432 | tf_op jit(solution)/shard_map/all_gather | solution.py:29
  116.9 9.6 %fusion.22 = bf16[640,2304]{1,0:T(8,128)(2,1)} fusion(bf16[640,1152]{1,0:T(8,128)(2,1)} %all-gather.6.cloned.1.call-done, bf16[1,1152,2304]{2,1,0:T(8,128)(2,1)} %all-gather.8.cloned.1.call-done, f32[2304]{0:T(1024)S(1)} %convert_reduce_fusion.1), kind=kOutput, calls=%fused_computation.30 | convolution fusion | flops 3412131840 | bytes 9741312 | tf_op jit(solution)/shard_map/dot_general | solution.py:107
  126.5 61.2 %all-gather.10.cloned.1.call-done = bf16[1,2304,1152]{2,1,0:T(8,128)(2,1)} async-done(((bf16[1,1152,1152]{2,1,0:T(8,128)(2,1)}), bf16[1,2304,1152]{2,1,0:T(8,128)(2,1)}) %all-gather.10.cloned.1.call-update) | async-done | bytes 5308432 | tf_op jit(solution)/shard_map/all_gather | solution.py:116
  187.8 8.5 %fusion.29 = bf16[640,1152]{1,0:T(8,128)(2,1)} fusion(bf16[640,2304]{1,0:T(8,128)(2,1)} %fusion.22, bf16[1,2304,1152]{2,1,0:T(8,128)(2,1)} %all-gather.10.cloned.1.call-done), kind=kOutput, calls=%fused_computation.35 | convolution fusion | flops 3398123520 | bytes 9732096 | tf_op jit(solution)/shard_map/dot_general | solution.py:118
  196.7 1.5 collective-permute-start
  198.2 2.3 collective-permute-start.1
  200.7 18.0 %all_gather.15 = bf16[1024,288]{0,1:T(8,128)(2,1)S(1)} all-gather(bf16[256,288]{0,1:T(8,128)(2,1)S(1)} %get-tuple-element.102), channel_id=1, replica_groups=mesh['groups'=2,'seq'=4,'exp'=2,'tp'=2] {'seq'}, dimensions={0}, use_global_device_ids=true | all-gather | bytes 737280 | tf_op jit(solution)/shard_map/all_gather | solution.py:47
  219.2 0.9 copy.31
  221.0 6.2 %collective-permute-done.2 = bf16[256,288]{0,1:T(8,128)(2,1)S(1)} collective-permute-done((bf16[256,288]{0,1:T(8,128)(2,1)S(1)}, bf16[256,288]{0,1:T(8,128)(2,1)S(1)}, u32[]{:S(2)}, u32[]{:S(2)}) %collective-permute-start.2) | collective-permute-done | bytes 147488 | tf_op jit(solution)/shard_map/ppermute | solution.py:18
  227.7 0.9 copy.30
  228.6 2.1 add_convert_fusion
  230.7 3.7 %all-to-all-start.1 = ((bf16[4,80,1152]{2,1,0:T(8,128)(2,1)}), bf16[4,80,1152]{2,1,0:T(8,128)(2,1)S(1)}, u32[]{:S(2)}, u32[]{:S(2)}) async-start(bf16[4,80,1152]{2,1,0:T(8,128)(2,1)} %bitcast.10), calls=%async_computation.2 | async-start | bytes 1474560 | tf_op jit(solution)/shard_map/all_to_all | solution.py:124
  234.4 6.9 %while.15 = (s32[]{:T(128)}, f32[4,256]{1,0:T(4,128)S(1)}, f32[4,256]{1,0:T(4,128)S(1)}, f32[4,256,72]{1,2,0:T(8,128)S(1)}, bf16[2,512,4,72]{1,3,2,0:T(8,128)(2,...) while((s32[]{:T(128)}, f32[4,256]{1,0:T(4,128)S(1)}, ...), condition=%wide.region_3.4_spmd.clone, body=%wide.region_0.3_spmd.clone.sunk | while | flops 155415552 | bytes 7685225 | solution.py:72
  234.4 1.5 bitcast_reduce_fusion.2
  236.3 1.5 convolution_add_fusion.2
  237.8 1.5 bitcast_reduce_fusion.2
  239.7 1.5 convolution_add_fusion.2
  241.9 7.0 %all-to-all-done.1 = bf16[4,80,1152]{2,1,0:T(8,128)(2,1)S(1)} async-done(((bf16[4,80,1152]{2,1,0:T(8,128)(2,1)}), bf16[4,80,1152]{2,1,0:T(8,128)(2,1)S(1)}, u32[]{:S(2)}, u32[]{:S(2)}) %all-to-all-start.1) | async-done | bytes 737312 | tf_op jit(solution)/shard_map/all_to_all | solution.py:124
  248.9 1.3 gather_fusion
  250.8 2.2 multiply_reduce_fusion
  (75 shorter events, 8.0 us)
Async XLA Ops:
  7.2 3.1 %copy-start = (bf16[128,1152]{1,0:T(8,128)(2,1)S(1)}, bf16[128,1152]{1,0:T(8,128)(2,1)}, u32[]{:S(2)}) copy-start(bf16[128,1152]{1,0:T(8,128)(2,1)} %param.21) | copy-start | bytes 884740
  7.2 37.7 %all-gather.6.cloned.1.call-start = ((), (), s32[]{:S(2)}) async-start(), calls=%async_computation.3 | async-start | bytes 2211840 | tf_op jit(solution)/shard_map/all_gather | solution.py:103
  36.0 1.5 copy-start.5
  36.0 80.9 %all-gather.8.cloned.1.call-start = ((), (), s32[]{:S(2)}) async-start(), calls=%async_computation.5 | async-start | bytes 7962624 | tf_op jit(solution)/shard_map/all_gather | solution.py:29
  36.7 151.0 %all-gather.10.cloned.1.call-start = ((), (), s32[]{:S(2)}) async-start(), calls=%async_computation.6 | async-start | bytes 7962624 | tf_op jit(solution)/shard_map/all_gather | solution.py:116
  37.5 191.1 %reduce-scatter.2.cloned.1.call-start = ((), (), s32[]{:S(2)}) async-start(), calls=%async_computation.4 | async-start | bytes 2211840 | tf_op jit(solution)/shard_map/reduce_scatter | solution.py:117
  126.5 69.9 %copy-start.8 = (s32[2]{0:T(128)S(1)}, s32[2]{0:T(128)}, u32[]{:S(2)}) copy-start(s32[2]{0:T(128)} %param.20) | copy-start | bytes 28
  126.5 70.0 %copy-start.1 = (bf16[256,288]{0,1:T(8,128)(2,1)S(1)}, bf16[256,288]{0,1:T(8,128)(2,1)}, u32[]{:S(2)}) copy-start(bf16[256,288]{0,1:T(8,128)(2,1)} %param.16) | copy-start | bytes 442372
  126.5 70.0 %copy-start.2 = (bf16[256,288]{0,1:T(8,128)(2,1)S(1)}, bf16[256,288]{0,1:T(8,128)(2,1)}, u32[]{:S(2)}) copy-start(bf16[256,288]{0,1:T(8,128)(2,1)} %param.18) | copy-start | bytes 442372
  126.5 70.1 %copy-start.3 = (bf16[256,288]{0,1:T(8,128)(2,1)S(1)}, bf16[256,288]{0,1:T(8,128)(2,1)}, u32[]{:S(2)}) copy-start(bf16[256,288]{0,1:T(8,128)(2,1)} %param.17) | copy-start | bytes 442372
  126.5 70.1 %copy-start.4 = (bf16[256,288]{0,1:T(8,128)(2,1)S(1)}, bf16[256,288]{0,1:T(8,128)(2,1)}, u32[]{:S(2)}) copy-start(bf16[256,288]{0,1:T(8,128)(2,1)} %param.19) | copy-start | bytes 442372
  196.3 23.7 %copy-start.7 = (f32[128,2]{0,1:T(2,128)S(1)}, f32[128,2]{0,1:T(2,128)}, u32[]{:S(2)}) copy-start(f32[128,2]{0,1:T(2,128)} %param.23) | copy-start | bytes 3076
  196.4 23.8 %copy-start.6 = (f32[1,1152]{1,0:T(1,128)S(1)}, f32[1,1152]{1,0:T(1,128)}, u32[]{:S(2)}) copy-start(f32[1,1152]{1,0:T(1,128)} %param.27) | copy-start | bytes 13828
  196.7 23.5 %collective-permute-start = (bf16[256,288]{0,1:T(8,128)(2,1)S(1)}, bf16[256,288]{0,1:T(8,128)(2,1)S(1)}, u32[]{:S(2)}, u32[]{:S(2)}) collective-permute-start(bf16[256,288]{0,1:T(8,128)(2,1)S(1)} %get-tuple-element.97), channel_id=1, source_target_pairs={{0,4},{4,8},{8,12},{12,0},{1,5},{5,9},{9,13},{13,1},{2,6},{6,10},{... | collective-permute-start | bytes 442376 | tf_op jit(solution)/shard_map/ppermute | solution.py:18
  198.2 22.8 %collective-permute-start.1 = (bf16[256,288]{0,1:T(8,128)(2,1)S(1)}, bf16[256,288]{0,1:T(8,128)(2,1)S(1)}, u32[]{:S(2)}, u32[]{:S(2)}) collective-permute-start(bf16[256,288]{0,1:T(8,128)(2,1)S(1)} %get-tuple-element.97), channel_id=1, source_target_pairs={{0,12},{4,0},{8,4},{12,8},{1,13},{5,1},{9,5},{13,9},{2,14},{6,2},{... | collective-permute-start | bytes 442376 | tf_op jit(solution)/shard_map/ppermute | solution.py:21
  220.2 7.0 %collective-permute-start.2 = (bf16[256,288]{0,1:T(8,128)(2,1)S(1)}, bf16[256,288]{0,1:T(8,128)(2,1)S(1)}, u32[]{:S(2)}, u32[]{:S(2)}) collective-permute-start(bf16[256,288]{0,1:T(8,128)(2,1)S(1)} %collective-permute-done), channel_id=1, source_target_pairs={{0,4},{4,8},{8,12},{12,0},{1,5},{5,9},{9,13},{13,1},{2,6},{6,10},{... | collective-permute-start | bytes 442376 | tf_op jit(solution)/shard_map/ppermute | solution.py:18
  230.7 18.2 %all-to-all-start.1 = ((bf16[4,80,1152]{2,1,0:T(8,128)(2,1)}), bf16[4,80,1152]{2,1,0:T(8,128)(2,1)S(1)}, u32[]{:S(2)}, u32[]{:S(2)}) async-start(bf16[4,80,1152]{2,1,0:T(8,128)(2,1)} %bitcast.10), calls=%async_computation.2 | async-start | bytes 1474560 | tf_op jit(solution)/shard_map/all_to_all | solution.py:124
Sparse Core Ops, SparseCore 0:
  36.1 8.7 all-gather.5
  46.4 70.4 all-gather.7
  118.5 69.2 all-gather.9
  196.5 8.8 reduce-scatter.1
